TPU v7x, 32 devices: a whole 2x2x4 slice. The times are simulated.
32 devices in a mesh: groups: 2 (over y), ctx: 8 (over z, x), head: 2 (over core).
Axes of the slice: x: 2, y: 2, z: 4, core: 2. Of those that a mesh axis runs over, the one named last changes fastest.
Arguments:
- query_latent: bfloat16 [16, 64, 576], P(('groups', 'ctx'), 'head'), parts along dimension 0, may hold values from -9 to 9
- latent_codes: bfloat16 [4096, 576], P(('groups', 'ctx')), parts along dimension 0, may hold values from -6 to 6
- latent_scales: float32 [4096, 9], P(('groups', 'ctx')), parts along dimension 0, may hold values from 0.5 to 2
- valid_lengths: int32 [16], P(('groups', 'ctx')), parts along dimension 0, may hold values from 1 to 256
- query_position: int32 [16], P('groups'), parts along dimension 0, may hold values from 0 to 2047
- value_up: bfloat16 [64, 512, 128], P('head'), may hold values from -1 to 1
- out_codes: bfloat16 [8192, 7168], P('head', 'ctx'), may hold values from -0.0625 to 0.0625
- out_scales: float32 [7168], P('ctx'), may hold values from 0.5 to 2
Outputs:
- attention: bfloat16 [16, 8192], P(('groups', 'ctx'), 'head'), parts along dimension 0
- projected: bfloat16 [16, 7168], P(('groups', 'head'), 'ctx'), parts along dimension 0
There are 2 independent parts, one for each index of `groups`. A program takes and returns all parts, laid end to end along the dimension named above; an argument that names none is the same for every part. Nothing has to cross between parts.
All inputs are finite; a program needn't handle non-finite values.
Results may differ from a plain program's by a relative error of at most 0.011.
Values may be sent and summed in bfloat16 or wider, within the bound.
A program may use at most 128 MiB of HBM per device.

v0:
```python
import jax
import jax.numpy as jnp
from jax import lax
from jax.sharding import PartitionSpec as P

LAT_NOPE = 512
ROPE = 64
QK_NOPE = 128


def shards(
    query_latent,
    latent_codes,
    latent_scales,
    valid_lengths,
    query_position,
    value_up,
    out_codes,
    out_scales,
):
    key_count, width = latent_codes.shape
    block_count = latent_scales.shape[1]
    latent = (
        (
            latent_codes.astype(jnp.float32).reshape(key_count, block_count, width // block_count)
            * latent_scales[:, :, None]
        )
        .reshape(key_count, width)
        .astype(jnp.bfloat16)
    )
    shard_index = lax.axis_index("ctx")
    local_slots = jnp.arange(key_count, dtype=jnp.int32)
    key_pos = shard_index * key_count + local_slots
    usable = local_slots < valid_lengths[0]
    softmax_scale = (QK_NOPE + ROPE) ** (-0.5)
    logits = (
        jnp.einsum(
            "qhc,kc->qhk",
            lax.all_gather(query_latent, "ctx", axis=0, tiled=True),
            latent,
            preferred_element_type=jnp.float32,
        )
        * softmax_scale
    )
    allowed = usable[None, :] & (key_pos[None, :] <= query_position[:, None])
    scores = jnp.where(allowed[:, None, :], logits, -jnp.inf)
    maxima = lax.pmax(jnp.max(scores, axis=2), "ctx")
    weights = jnp.exp(scores - maxima[:, :, None])
    totals = jnp.sum(weights, axis=2)
    latent_mix = jnp.einsum(
        "qhk,kd->qhd",
        weights.astype(jnp.bfloat16),
        latent[:, :LAT_NOPE],
        preferred_element_type=jnp.float32,
    ).astype(jnp.bfloat16)
    values = jnp.einsum("qhd,hdv->qhv", latent_mix, value_up, preferred_element_type=jnp.float32)
    queries, head_count, value_width = values.shape
    numerators = values.reshape(queries, head_count * value_width)
    own_rows = query_latent.shape[0]
    numer_sum, denom_sum = lax.psum((numerators, totals), "ctx")
    attn_all = (
        (numer_sum.reshape(queries, head_count, value_width) / denom_sum[:, :, None])
        .reshape(queries, head_count * value_width)
        .astype(jnp.bfloat16)
    )
    attn_home = lax.dynamic_slice_in_dim(attn_all, shard_index * own_rows, own_rows, 0)
    summed = lax.psum_scatter(
        jnp.dot(attn_all, out_codes, preferred_element_type=jnp.float32),
        "head",
        scatter_dimension=0,
        tiled=True,
    )
    projected = (summed * out_scales[None, :]).astype(jnp.bfloat16)
    return (attn_home, projected)


def solution(mesh):
    return jax.shard_map(
        shards,
        mesh=mesh,
        in_specs=(
            P(("groups", "ctx"), "head", None),
            P(("groups", "ctx"), None),
            P(("groups", "ctx"), None),
            P(("groups", "ctx")),
            P("groups"),
            P("head", None, None),
            P("head", "ctx"),
            P("ctx"),
        ),
        out_specs=(P(("groups", "ctx"), "head"), P(("groups", "head"), "ctx")),
        check_vma=False,
    )
```

profile of v0, /device:TPU:0, one launch (start us, length us, event | category | flops | bytes accessed | tf_op | source)
XLA Modules:
  0.0 152.8 jit_solution(15896738344117808828)
XLA Ops:
  7.2 0.0 copy-start.1
  7.2 0.0 all-reduce.3.cloned.1.call-start
  7.9 32.9 %all_gather.3 = bf16[8,32,576]{2,1,0:T(8,128)(2,1)S(1)} all-gather(bf16[1,32,576]{2,1,0:T(8,128)(2,1)} %param.8), channel_id=1, replica_groups=mesh['groups'=2,'ctx'=8,'head'=2] {'ctx'}, dimensions={0}, use_global_device_ids=true | all-gather | bytes 331776 | tf_op jit(solution)/shard_map/all_gather | solution.py:39
  40.8 0.0 copy-start
  40.8 1.0 fusion.2
  41.8 0.7 compare_and_fusion
  42.6 0.3 fusion.10
  42.9 21.4 %pmax.7 = f32[8,32]{1,0:T(8,128)S(1)} all-reduce(f32[8,32]{1,0:T(8,128)S(1)} %get-tuple-element.4), channel_id=1, replica_groups=mesh['groups'=2,'ctx'=8,'head'=2] {'ctx'}, use_global_device_ids=true, to_apply=%region_1.2 | all-reduce | flops 256 | bytes 2048 | tf_op jit(solution)/shard_map/pmax | solution.py:47
  64.3 0.2 fusion.4
  64.5 3.7 %convolution_bitcast_fusion = f32[8,4096]{1,0:T(8,128)} fusion(bf16[32,512,128]{2,1,0:T(8,128)(2,1)} %param.13, bf16[256,576]{0,1:T(8,128)(2,1)S(1)} %fusion.2, bf16[8,32,256]{2,1,0:T(8,128)(2,1)S(1)} %get-tuple-element.3), kind=kOutput, calls=%fused_computation | convolution fusion | flops 100794368 | bytes 4718592 | tf_op jit(solution)/shard_map/qhd,hdv->qhv/dot_general | solution.py:56
  68.2 0.0 all-reduce.3.cloned.1.call-update
  68.2 17.1 %psum.15 = f32[8,32]{1,0:T(8,128)S(1)} all-reduce(f32[8,32]{1,0:T(8,128)S(1)} %get-tuple-element.2), channel_id=1, replica_groups=mesh['groups'=2,'ctx'=8,'head'=2] {'ctx'}, use_global_device_ids=true, to_apply=%region_4.5 | all-reduce | flops 256 | bytes 2048 | tf_op jit(solution)/shard_map/psum | solution.py:60
  85.4 0.1 copy.10
  85.4 0.0 copy-done.1
  85.4 0.6 dynamic-slice
  86.7 49.4 %all-reduce.3.cloned.1.call-done = f32[8,4096]{1,0:T(8,128)} async-done(((f32[8,4096]{1,0:T(8,128)}), f32[8,4096]{1,0:T(8,128)}) %all-reduce.3.cloned.1.call-update) | async-done | bytes 131088 | tf_op jit(solution)/shard_map/psum | solution.py:60
  136.1 1.0 fusion.6
  137.1 0.6 constant_dynamic-slice_fusion
  137.8 4.1 %fusion.11 = f32[8,896]{1,0:T(8,128)S(1)} fusion(bf16[8,4096]{1,0:T(8,128)(2,1)S(1)} %fusion.6, bf16[4096,896]{1,0:T(8,128)(2,1)} %param.14), kind=kOutput, calls=%fused_computation.22 | convolution fusion | flops 58720256 | bytes 7434240 | tf_op jit(solution)/shard_map/dot_general | solution.py:68
  141.9 3.4 %all-reduce = f32[8,896]{1,0:T(8,128)S(1)} all-reduce(f32[8,896]{1,0:T(8,128)S(1)} %fusion.11), channel_id=2, replica_groups=mesh['groups'=2,'ctx'=8,'head'=2] {'head'}, use_global_device_ids=true, to_apply=%region_5.6.clone | all-reduce | flops 7168 | bytes 57344
  145.3 0.0 copy-done
  145.3 0.6 fusion.9
  (2 shorter events, 0.0 us)
Async XLA Ops:
  7.2 78.3 %copy-start.1 = (u32[32]{0:T(128)S(1)}, u32[32]{0:T(128)}, u32[]{:S(2)}) copy-start(u32[32]{0:T(128)} %constant.22) | copy-start | bytes 388
  7.2 129.0 %all-reduce.3.cloned.1.call-start = ((), (), s32[]{:S(2)}) async-start(), calls=%async_computation | async-start | bytes 262144 | tf_op jit(solution)/shard_map/psum | solution.py:60
  40.8 104.5 %copy-start = (f32[896]{0:T(1024)S(1)}, f32[896]{0:T(1024)}, u32[]{:S(2)}) copy-start(f32[896]{0:T(1024)} %param.15) | copy-start | bytes 10756
Sparse Core Ops, SparseCore 0:
  68.3 67.7 all-reduce.2
where the time goes:
time: 153 us
  blocking collectives  74.8 us (49%)
  waiting for transfers between devices  49.5 us (32%)
  between operations  15.4 us (10%)
  matrix products  8.16 us (5%)
  other arithmetic  3.58 us (2%)
    psum x1, waiting for transfers between devices, shards(): numer_sum, denom_sum = lax.psum((numerators, totals), 'ctx')  49.4 us
    all_gather x1, blocking collectives, shards(): lax.all_gather(query_latent, 'ctx', axis=0, tiled=True)  32.9 us
    pmax x1, blocking collectives, shards(): maxima = lax.pmax(jnp.max(scores, axis=2), 'ctx')  21.4 us
    psum x1, blocking collectives, shards(): numer_sum, denom_sum = lax.psum((numerators, totals), 'ctx')  17.1 us
    dot_general x1, matrix products, shards(): jnp.dot(attn_all, out_codes, preferred_element_type=jnp.float32)  4.13 us
    dot_general x1, matrix products, shards(): jnp.einsum('qhd,hdv->qhv', latent_mix, value_up, preferred_element_type=j...  3.69 us
    unnamed x1, blocking collectives  3.4 us
  transfers between devices with their start and end apart: 1, of which 1 were waited for; matrix products, arithmetic and copies ran while one was open for 0% of the time, Pallas kernels for 0%

commit v1 on v0

--- a/solution.py
+++ b/solution.py
@@ -1,11 +1,18 @@
+import functools
+
 import jax
 import jax.numpy as jnp
 from jax import lax
+from jax.experimental import pallas as pl
+from jax.experimental.pallas import tpu as pltpu
 from jax.sharding import PartitionSpec as P
 
 LAT_NOPE = 512
 ROPE = 64
 QK_NOPE = 128
+LANES = 128
+MASKED = -1e30
+MESH = pl.DeviceIdType.MESH
 
 
 def shards(
@@ -74,9 +81,330 @@
     return (attn_home, projected)
 
 
+def fused(
+    n,
+    heads,
+    valid_ref,
+    qpos_ref,
+    query_hbm,
+    codes_hbm,
+    scales_hbm,
+    up_hbm,
+    out_hbm,
+    out_scales_ref,
+    attn_ref,
+    proj_ref,
+    q_all,
+    codes,
+    scales,
+    up,
+    outw,
+    latent,
+    mix,
+    stat_m,
+    stat_l,
+    num_send,
+    num_recv,
+    st_send,
+    st_recv,
+    att_all,
+    part,
+    part_recv,
+    in_sem,
+    up_sem,
+    out_sem,
+    q_send,
+    q_recv,
+    num_ssem,
+    num_rsem,
+    st_ssem,
+    st_rsem,
+    att_ssem,
+    att_rsem,
+    part_ssem,
+    part_rsem,
+):
+    me = lax.axis_index("ctx")
+    hd = lax.axis_index("head")
+    side = lax.rem(me, 2)
+    partner = me + 1 - 2 * side
+    half = n // 2
+    tokens, head_count, width = q_all.shape
+    keys = codes.shape[0]
+    nope = mix.shape[0] * LANES
+    vhead = up.shape[2]
+    per = head_count // n
+    cols = per * vhead
+
+    def at(k):
+        return lax.rem(me + k + n, n)
+
+    barrier = pltpu.get_barrier_semaphore()
+    for k in range(1, n):
+        pl.semaphore_signal(barrier, inc=1, device_id={"ctx": at(k)}, device_id_type=MESH)
+    for k in range(1, heads):
+        pl.semaphore_signal(
+            barrier, inc=1, device_id={"head": lax.rem(hd + k, heads)}, device_id_type=MESH
+        )
+
+    own_q = pltpu.make_async_copy(query_hbm.at[0], q_all.at[me], in_sem.at[0])
+    own_q.start()
+    codes_in = pltpu.make_async_copy(codes_hbm, codes, in_sem.at[1])
+    codes_in.start()
+    scales_in = pltpu.make_async_copy(scales_hbm, scales, in_sem.at[2])
+    scales_in.start()
+    up_in = []
+    for g in range(n):
+        rows = pl.ds(g * per, per)
+        up_in.append(pltpu.make_async_copy(up_hbm.at[rows], up.at[rows], up_sem.at[g]))
+        up_in[-1].start()
+    out_in = []
+    for g in range(n):
+        rows = pl.ds(g * cols, cols)
+        out_in.append(pltpu.make_async_copy(out_hbm.at[rows], outw.at[rows], out_sem.at[g]))
+        out_in[-1].start()
+
+    own_q.wait()
+    pl.semaphore_wait(barrier, n - 1 + heads - 1)
+
+    def send_q(token, target, index):
+        copy = pltpu.make_async_remote_copy(
+            src_ref=q_all.at[token],
+            dst_ref=q_all.at[token],
+            send_sem=q_send.at[index],
+            recv_sem=q_recv.at[index],
+            device_id={"ctx": target},
+            device_id_type=MESH,
+        )
+        copy.start()
+        return copy
+
+    sent = [send_q(me, partner, half)]
+    direct = [send_q(me, at(2 * k), k) for k in range(1, half)]
+
+    codes_in.wait()
+    scales_in.wait()
+    block = width // scales.shape[1]
+    lane = lax.broadcasted_iota(jnp.int32, (keys, LANES), 1)
+    for start in range(0, width, LANES):
+        span = min(LANES, width - start)
+        first = start // block
+        scale = jnp.broadcast_to(scales[:, first : first + 1], (keys, LANES))
+        for b in range(1, span // block):
+            scale = jnp.where(lane >= b * block, scales[:, first + b : first + b + 1], scale)
+        latent[:, start : start + span] = (
+            codes[:, start : start + span].astype(jnp.float32) * scale[:, :span]
+        ).astype(jnp.bfloat16)
+
+    for k in range(1, half):
+        direct[k - 1].wait_recv()
+        sent.append(send_q(at(-2 * k), partner, half + k))
+    for copy in sent:
+        copy.wait_recv()
+
+    softmax_scale = (QK_NOPE + ROPE) ** (-0.5)
+    logits = (
+        lax.dot_general(
+            q_all[...].reshape(tokens * head_count, width),
+            latent[...],
+            (((1,), (1,)), ((), ())),
+            preferred_element_type=jnp.float32,
+        )
+        * softmax_scale
+    )
+    slot = lax.broadcasted_iota(jnp.int32, (head_count, keys), 1)
+    weights = []
+    for t in range(tokens):
+        limit = jnp.minimum(valid_ref[0], qpos_ref[t] - me * keys + 1)
+        allowed = slot < limit
+        rows = slice(t * head_count, (t + 1) * head_count)
+        scores = jnp.where(allowed, logits[rows], MASKED)
+        top = jnp.max(scores, axis=1, keepdims=True)
+        weight = jnp.where(allowed, jnp.exp(scores - top), 0.0)
+        stat_m[rows, :] = jnp.broadcast_to(top, (head_count, LANES))
+        stat_l[rows, :] = jnp.broadcast_to(jnp.sum(weight, axis=1, keepdims=True), (head_count, LANES))
+        weights.append(weight.astype(jnp.bfloat16))
+    mixed_all = jnp.dot(
+        jnp.concatenate(weights, axis=0), latent[:, :nope], preferred_element_type=jnp.float32
+    )
+    for c in range(mix.shape[0]):
+        mix[c] = mixed_all[:, c * LANES : (c + 1) * LANES]
+
+    tile_lane = lax.broadcasted_iota(jnp.int32, (tokens, LANES), 1)
+    for g in range(n):
+        up_in[g].wait()
+        stat = jnp.zeros((tokens, LANES), jnp.float32)
+        for j in range(per):
+            h = g * per + j
+            rows = pl.ds(h, tokens, stride=head_count)
+            mixed = jnp.concatenate(
+                [mix[c, rows, :] for c in range(mix.shape[0])], axis=1
+            ).astype(jnp.bfloat16)
+            num_send[g, :, j * vhead : (j + 1) * vhead] = jnp.dot(
+                mixed, up[h], preferred_element_type=jnp.float32
+            ).astype(jnp.bfloat16)
+            stat = jnp.where(tile_lane == j, stat_m[rows, :], stat)
+            stat = jnp.where(tile_lane == per + j, stat_l[rows, :], stat)
+        st_send[g] = stat
+
+    moved = []
+    for k in range(1, n):
+        target = at(k)
+        for src, dst, ssem, rsem in (
+            (st_send, st_recv, st_ssem, st_rsem),
+            (num_send, num_recv, num_ssem, num_rsem),
+        ):
+            copy = pltpu.make_async_remote_copy(
+                src_ref=src.at[target],
+                dst_ref=dst.at[k],
+                send_sem=ssem.at[k],
+                recv_sem=rsem.at[k],
+                device_id={"ctx": target},
+                device_id_type=MESH,
+            )
+            copy.start()
+            moved.append(copy)
+    for copy in direct + sent:
+        copy.wait_send()
+    for copy in moved:
+        copy.wait_recv()
+
+    stats = [st_send[me]] + [st_recv[k] for k in range(1, n)]
+    nums = [num_send[me]] + [num_recv[k] for k in range(1, n)]
+    top = functools.reduce(jnp.maximum, stats)
+    factors = [jnp.exp(s - top) for s in stats]
+    pieces = []
+    for j in range(per):
+        total = jnp.zeros((tokens, 1), jnp.float32)
+        value = jnp.zeros((tokens, vhead), jnp.float32)
+        for s, f, v in zip(stats, factors, nums):
+            factor = f[:, j : j + 1]
+            total += factor * s[:, per + j : per + j + 1]
+            value += factor * v[:, j * vhead : (j + 1) * vhead].astype(jnp.float32)
+        pieces.append((value / total).astype(jnp.bfloat16))
+    att_all[me] = jnp.concatenate(pieces, axis=1)
+
+    shared = []
+    for k in range(1, n):
+        copy = pltpu.make_async_remote_copy(
+            src_ref=att_all.at[me],
+            dst_ref=att_all.at[me],
+            send_sem=att_ssem.at[k],
+            recv_sem=att_rsem.at[k],
+            device_id={"ctx": at(k)},
+            device_id_type=MESH,
+        )
+        copy.start()
+        shared.append(copy)
+    for copy in moved:
+        copy.wait_send()
+    for copy in out_in:
+        copy.wait()
+    columns = outw.shape[1]
+    acc = jnp.zeros((tokens, columns), jnp.float32)
+    for k in range(n):
+        if k:
+            shared[k - 1].wait_recv()
+        g = at(-k)
+        acc += jnp.dot(
+            att_all[g],
+            outw[pl.ds(pl.multiple_of(g * cols, cols), cols), :],
+            preferred_element_type=jnp.float32,
+        )
+    rows = tokens // heads
+    for i in range(heads):
+        part[i] = acc[i * rows : (i + 1) * rows]
+    swapped = []
+    for k in range(1, heads):
+        other = lax.rem(hd + k, heads)
+        copy = pltpu.make_async_remote_copy(
+            src_ref=part.at[other],
+            dst_ref=part_recv.at[k],
+            send_sem=part_ssem.at[k],
+            recv_sem=part_rsem.at[k],
+            device_id={"head": other},
+            device_id_type=MESH,
+        )
+        copy.start()
+        swapped.append(copy)
+    row = lax.broadcasted_iota(jnp.int32, (tokens, cols), 0)
+    for g in range(n):
+        attn_ref[:, g * cols : (g + 1) * cols] = jnp.sum(
+            jnp.where(row == me, att_all[g].astype(jnp.float32), 0.0), axis=0, keepdims=True
+        ).astype(jnp.bfloat16)
+    summed = part[hd]
+    for k in range(1, heads):
+        swapped[k - 1].wait_recv()
+        summed += part_recv[k]
+    proj_ref[...] = (summed * out_scales_ref[...]).astype(jnp.bfloat16)
+    for copy in shared + swapped:
+        copy.wait_send()
+
+
+def block(n, heads, *args):
+    query, codes, scales, valid, qpos, up, outw, out_scales = args
+    own, head_count, width = query.shape
+    tokens = own * n
+    fits = own == 1 and n % 2 == 0 and head_count % n == 0 and tokens % (4 * heads) == 0
+    if not fits:
+        return shards(*args)
+    keys = codes.shape[0]
+    vhead = up.shape[2]
+    per = head_count // n
+    cols = per * vhead
+    columns = outw.shape[1]
+    anywhere = pl.BlockSpec(memory_space=pl.ANY)
+    vmem = pl.BlockSpec(memory_space=pltpu.VMEM)
+    smem = pl.BlockSpec(memory_space=pltpu.SMEM)
+    dma = pltpu.SemaphoreType.DMA
+    return pl.pallas_call(
+        functools.partial(fused, n, heads),
+        out_shape=(
+            jax.ShapeDtypeStruct((own, head_count * vhead), jnp.bfloat16),
+            jax.ShapeDtypeStruct((tokens // heads, columns), jnp.bfloat16),
+        ),
+        in_specs=[smem, smem] + [anywhere] * 5 + [vmem],
+        out_specs=(vmem, vmem),
+        scratch_shapes=[
+            pltpu.VMEM((tokens, head_count, width), jnp.bfloat16),
+            pltpu.VMEM(codes.shape, jnp.bfloat16),
+            pltpu.VMEM(scales.shape, jnp.float32),
+            pltpu.VMEM(up.shape, jnp.bfloat16),
+            pltpu.VMEM(outw.shape, jnp.bfloat16),
+            pltpu.VMEM((keys, width), jnp.bfloat16),
+            pltpu.VMEM((LAT_NOPE // LANES, tokens * head_count, LANES), jnp.float32),
+            pltpu.VMEM((tokens * head_count, LANES), jnp.float32),
+            pltpu.VMEM((tokens * head_count, LANES), jnp.float32),
+            pltpu.VMEM((n, tokens, cols), jnp.bfloat16),
+            pltpu.VMEM((n, tokens, cols), jnp.bfloat16),
+            pltpu.VMEM((n, tokens, LANES), jnp.float32),
+            pltpu.VMEM((n, tokens, LANES), jnp.float32),
+            pltpu.VMEM((n, tokens, cols), jnp.bfloat16),
+            pltpu.VMEM((heads, tokens // heads, columns), jnp.float32),
+            pltpu.VMEM((heads, tokens // heads, columns), jnp.float32),
+            dma((3,)),
+            dma((n,)),
+            dma((n,)),
+            dma((n,)),
+            dma((n,)),
+            dma((n,)),
+            dma((n,)),
+            dma((n,)),
+            dma((n,)),
+            dma((n,)),
+            dma((n,)),
+            dma((heads,)),
+            dma((heads,)),
+        ],
+        compiler_params=pltpu.CompilerParams(collective_id=0, has_side_effects=True),
+        name="mla_block",
+    )(valid, qpos, query, codes, scales, up, outw, out_scales.reshape(1, -1))
+
+
 def solution(mesh):
+    ctx, heads = mesh.shape["ctx"], mesh.shape["head"]
     return jax.shard_map(
-        shards,
+        functools.partial(block, ctx, heads),
         mesh=mesh,
         in_specs=(
             P(("groups", "ctx"), "head", None),

time: 153 us -> 40.2 us (0.26)
  blocking collectives: 74.8 us -> 0 us
  waiting for transfers between devices: 49.5 us -> 0 us
  Pallas kernels: 0 us -> 31.2 us
  between operations: 15.4 us -> 1.29 us
  matrix products: 8.16 us -> 0 us
  local copies, waits for them, and re-layouts: 1.3 us -> 7.22 us
  other arithmetic: 3.58 us -> 0 us
    psum x1 -> x0, waiting for transfers between devices: 49.4 us -> none  [shards(): numer_sum, denom_sum = lax.psum((numerators, totals), 'ctx')]
    all_gather x1 -> x0, blocking collectives: 32.9 us -> none  [shards(): lax.all_gather(query_latent, 'ctx', axis=0, tiled=True)]
    pallas_call x0 -> x1, Pallas kernels: none -> 31.2 us  [block(): pl.pallas_call(functools.partial(fused, n, heads), out_shape=(jax.ShapeDt...]
    pmax x1 -> x0, blocking collectives: 21.4 us -> none  [shards(): maxima = lax.pmax(jnp.max(scores, axis=2), 'ctx')]
    psum x1 -> x0, blocking collectives: 17.1 us -> none  [shards(): numer_sum, denom_sum = lax.psum((numerators, totals), 'ctx')]
    dot_general x3 -> x0, matrix products: 8.16 us -> none  [the longest x1 4.13 us: shards(): jnp.dot(attn_all, out_codes, preferred_element_type=jnp.float32)]
    unnamed x5 -> x4, local copies, waits for them, and re-layouts: 0.59 us -> 5.95 us
    unnamed x1 -> x0, blocking collectives: 3.4 us -> none
  transfers between devices with their start and end apart: 1 -> 0, of which waited for: 1 -> 0; matrix products, arithmetic and copies ran while one was open for 0% -> 0% of each run, Pallas kernels for 0% -> 0%
where the time goes in v1:
time: 40.2 us; the launch traced here: 39.7 us
  Pallas kernels  31.2 us (78%)
  local copies, waits for them, and re-layouts  7.22 us (18%)
  between operations  1.29 us (3%)
    pallas_call x1, Pallas kernels, block(): pl.pallas_call(functools.partial(fused, n, heads), out_shape=(jax.ShapeDt...  31.2 us
    unnamed x4, local copies, waits for them, and re-layouts  5.95 us
    reshape x1, local copies, waits for them, and re-layouts, block(): out_scales.reshape(1, -1)  1.27 us

profile of v1, /device:TPU:0, one launch (start us, length us, event | category | flops | bytes accessed | tf_op | source)
XLA Modules:
  0.0 39.7 jit_solution(17696812833705084053)
XLA Ops:
  1.3 1.3 %reshape.7.out_scales_ref = f32[1,896]{1,0:T(1,128)} reshape(f32[896]{0:T(1024)} %param.15) | data formatting | bytes 7168 | tf_op jit(solution)/shard_map/reshape | solution.py:401
  2.5 1.5 %copy.11.scales_hbm = f32[256,9]{1,0:T(8,128)} copy(f32[256,9]{0,1:T(8,128)} %param.10) | data formatting | bytes 18432 | tf_op args[2]
  4.0 1.8 %copy.10.codes_hbm = bf16[256,576]{1,0:T(8,128)(2,1)} copy(bf16[256,576]{0,1:T(8,128)(2,1)} %param.9) | data formatting | bytes 589824 | tf_op args[1]
  5.9 31.2 %mla_block.1 = (bf16[1,4096]{1,0:T(2,128)(2,1)}, bf16[4,896]{1,0:T(4,128)(2,1)}) custom-call(s32[1]{0:T(128)S(6)} %copy.14.valid_ref, s32[8]{0:T(128)} %qpos_ref.1, bf16[1,32,576]{2,1,0:T(8,128)(2,1)} %query_hbm.1, bf16[256,576]{1,0:T(8,128)(2,1)} %copy.10.codes_hbm, f32[256,9]{1,0:T(8,128)} %copy.11.scales_hbm, bf16[32,512,128]{2,1,0:T(8,128)(2,1)} %up_hbm.1, ...), custom_call_target="tpu_custom_call" | custom-call | tf_op jit(solution)/shard_map/mla_block/pallas_call | solution.py:360
  37.0 1.3 %copy.15 = bf16[1,4096]{1,0:T(2,128)(2,1)} copy(bf16[1,4096]{1,0:T(2,128)(2,1)} %get-tuple-element.4) | data formatting | bytes 16384
  38.4 1.3 %copy.16 = bf16[4,896]{1,0:T(4,128)(2,1)} copy(bf16[4,896]{1,0:T(4,128)(2,1)} %get-tuple-element.5) | data formatting | bytes 14336

commit v2 on v1

--- a/solution.py
+++ b/solution.py
@@ -91,7 +91,6 @@
     scales_hbm,
     up_hbm,
     out_hbm,
-    out_scales_ref,
     attn_ref,
     proj_ref,
     q_all,
@@ -130,7 +129,7 @@
     partner = me + 1 - 2 * side
     half = n // 2
     tokens, head_count, width = q_all.shape
-    keys = codes.shape[0]
+    keys = codes.shape[1]
     nope = mix.shape[0] * LANES
     vhead = up.shape[2]
     per = head_count // n
@@ -184,17 +183,10 @@
 
     codes_in.wait()
     scales_in.wait()
-    block = width // scales.shape[1]
-    lane = lax.broadcasted_iota(jnp.int32, (keys, LANES), 1)
-    for start in range(0, width, LANES):
-        span = min(LANES, width - start)
-        first = start // block
-        scale = jnp.broadcast_to(scales[:, first : first + 1], (keys, LANES))
-        for b in range(1, span // block):
-            scale = jnp.where(lane >= b * block, scales[:, first + b : first + b + 1], scale)
-        latent[:, start : start + span] = (
-            codes[:, start : start + span].astype(jnp.float32) * scale[:, :span]
-        ).astype(jnp.bfloat16)
+    block = width // scales.shape[0]
+    for b in range(scales.shape[0]):
+        rows = slice(b * block, (b + 1) * block)
+        latent[rows, :] = (codes[rows, :].astype(jnp.float32) * scales[b : b + 1, :]).astype(jnp.bfloat16)
 
     for k in range(1, half):
         direct[k - 1].wait_recv()
@@ -204,10 +196,9 @@
 
     softmax_scale = (QK_NOPE + ROPE) ** (-0.5)
     logits = (
-        lax.dot_general(
+        jnp.dot(
             q_all[...].reshape(tokens * head_count, width),
             latent[...],
-            (((1,), (1,)), ((), ())),
             preferred_element_type=jnp.float32,
         )
         * softmax_scale
@@ -224,8 +215,11 @@
         stat_m[rows, :] = jnp.broadcast_to(top, (head_count, LANES))
         stat_l[rows, :] = jnp.broadcast_to(jnp.sum(weight, axis=1, keepdims=True), (head_count, LANES))
         weights.append(weight.astype(jnp.bfloat16))
-    mixed_all = jnp.dot(
-        jnp.concatenate(weights, axis=0), latent[:, :nope], preferred_element_type=jnp.float32
+    mixed_all = lax.dot_general(
+        jnp.concatenate(weights, axis=0),
+        latent[:nope, :],
+        (((1,), (1,)), ((), ())),
+        preferred_element_type=jnp.float32,
     )
     for c in range(mix.shape[0]):
         mix[c] = mixed_all[:, c * LANES : (c + 1) * LANES]
@@ -331,12 +325,12 @@
     for g in range(n):
         attn_ref[:, g * cols : (g + 1) * cols] = jnp.sum(
             jnp.where(row == me, att_all[g].astype(jnp.float32), 0.0), axis=0, keepdims=True
-        ).astype(jnp.bfloat16)
+        )
     summed = part[hd]
     for k in range(1, heads):
         swapped[k - 1].wait_recv()
         summed += part_recv[k]
-    proj_ref[...] = (summed * out_scales_ref[...]).astype(jnp.bfloat16)
+    proj_ref[...] = summed
     for copy in shared + swapped:
         copy.wait_send()
 
@@ -357,21 +351,21 @@
     vmem = pl.BlockSpec(memory_space=pltpu.VMEM)
     smem = pl.BlockSpec(memory_space=pltpu.SMEM)
     dma = pltpu.SemaphoreType.DMA
-    return pl.pallas_call(
+    attention, summed = pl.pallas_call(
         functools.partial(fused, n, heads),
         out_shape=(
-            jax.ShapeDtypeStruct((own, head_count * vhead), jnp.bfloat16),
-            jax.ShapeDtypeStruct((tokens // heads, columns), jnp.bfloat16),
+            jax.ShapeDtypeStruct((own, head_count * vhead), jnp.float32),
+            jax.ShapeDtypeStruct((tokens // heads, columns), jnp.float32),
         ),
-        in_specs=[smem, smem] + [anywhere] * 5 + [vmem],
+        in_specs=[smem, smem] + [anywhere] * 5,
         out_specs=(vmem, vmem),
         scratch_shapes=[
             pltpu.VMEM((tokens, head_count, width), jnp.bfloat16),
-            pltpu.VMEM(codes.shape, jnp.bfloat16),
-            pltpu.VMEM(scales.shape, jnp.float32),
+            pltpu.VMEM((width, keys), jnp.bfloat16),
+            pltpu.VMEM(scales.shape[::-1], jnp.float32),
             pltpu.VMEM(up.shape, jnp.bfloat16),
             pltpu.VMEM(outw.shape, jnp.bfloat16),
-            pltpu.VMEM((keys, width), jnp.bfloat16),
+            pltpu.VMEM((width, keys), jnp.bfloat16),
             pltpu.VMEM((LAT_NOPE // LANES, tokens * head_count, LANES), jnp.float32),
             pltpu.VMEM((tokens * head_count, LANES), jnp.float32),
             pltpu.VMEM((tokens * head_count, LANES), jnp.float32),
@@ -398,7 +392,9 @@
         ],
         compiler_params=pltpu.CompilerParams(collective_id=0, has_side_effects=True),
         name="mla_block",
-    )(valid, qpos, query, codes, scales, up, outw, out_scales.reshape(1, -1))
+    )(valid, qpos, query, codes.T, scales.T, up, outw)
+    projected = (summed * out_scales[None, :]).astype(jnp.bfloat16)
+    return attention.astype(jnp.bfloat16), projected
 
 
 def solution(mesh):

time: 40.2 us -> 35.4 us (0.88)
  local copies, waits for them, and re-layouts: 7.22 us -> 0.01 us
  other arithmetic: 0 us -> 2.65 us
    unnamed x4 -> x2, local copies, waits for them, and re-layouts: 5.95 us -> 0.01 us
    convert_element_type x0 -> x2, other arithmetic: none -> 2.65 us  [the longest x1 1.34 us: block(): return (attention.astype(jnp.bfloat16), projected)]
    reshape x1 -> x0, local copies, waits for them, and re-layouts: 1.27 us -> none  [block(): out_scales.reshape(1, -1)]
where the time goes in v2:
time: 35.4 us; the launch traced here: 35 us
  Pallas kernels  31.1 us (88%)
  other arithmetic  2.65 us (7%)
  between operations  1.31 us (4%)
    pallas_call x1, Pallas kernels, block(): pl.pallas_call(functools.partial(fused, n, heads), out_shape=(jax.ShapeDt...  31.1 us
    convert_element_type x1, other arithmetic, block(): return (attention.astype(jnp.bfloat16), projected)  1.34 us
    convert_element_type x1, other arithmetic, block(): projected = (summed * out_scales[None, :]).astype(jnp.bfloat16)  1.31 us

profile of v2, /device:TPU:0, one launch (start us, length us, event | category | flops | bytes accessed | tf_op | source)
XLA Modules:
  0.0 35.0 jit_solution(7563698036203872743)
XLA Ops:
  0.6 0.0 copy-start
  1.3 31.1 %mla_block.1 = (f32[1,4096]{1,0:T(1,128)}, f32[4,896]{1,0:T(4,128)}) custom-call(s32[1]{0:T(128)S(6)} %copy.10.valid_ref, s32[8]{0:T(128)} %qpos_ref.1, bf16[1,32,576]{2,1,0:T(8,128)(2,1)} %query_hbm.1, bf16[576,256]{1,0:T(8,128)(2,1)} %bitcast.2, f32[9,256]{1,0:T(8,128)} %bitcast.3, bf16[32,512,128]{2,1,0:T(8,128)(2,1)} %up_hbm.1, bf16[4096,896]{1,0:T(8,128)(2,1)} %out_hbm.1), custom_call_target="tpu_custom_call" | custom-call | tf_op jit(solution)/shard_map/mla_block/pallas_call | solution.py:354
  32.4 1.3 %convert_element_type.6 = bf16[1,4096]{1,0:T(2,128)(2,1)} convert(f32[1,4096]{1,0:T(1,128)} %get-tuple-element.4) | non-fusion elementwise | flops 4096 | bytes 24576 | tf_op jit(solution)/shard_map/convert_element_type | solution.py:397
  33.7 0.0 copy-done
  33.7 1.3 %multiply_convert_fusion = bf16[4,896]{1,0:T(4,128)(2,1)} fusion(f32[4,896]{1,0:T(4,128)} %get-tuple-element.5, f32[896]{0:T(1024)S(1)} %copy-done), kind=kLoop, calls=%fused_computation | loop fusion | flops 7168 | bytes 25088 | tf_op jit(solution)/shard_map/convert_element_type | solution.py:396
Async XLA Ops:
  0.6 33.1 %copy-start = (f32[896]{0:T(1024)S(1)}, f32[896]{0:T(1024)}, u32[]{:S(2)}) copy-start(f32[896]{0:T(1024)} %param.15) | copy-start | bytes 10756
